TPU v7x, 8 devices: a whole 2x2x1 slice. The times are simulated.
8 devices in a mesh: data: 2 (over z, y), tp: 4 (over x, core).
Axes of the slice: x: 2, y: 2, z: 1, core: 2. Of those that a mesh axis runs over, the one named last changes fastest.
Arguments:
- x: bfloat16 [2048, 49152], P('data', 'tp'), parts along dimension 0
- w: bfloat16 [49152, 12288], P('tp')
- lengths: int32 [8], P('data'), parts along dimension 0
Outputs:
- output: bfloat16 [2048, 12288], P('data'), parts along dimension 0
There are 2 independent parts. A program takes and returns all parts, laid end to end along the dimension named above; an argument that names none is the same for every part.
All inputs are finite; a program needn't handle non-finite values.
Results may differ from a plain program's by a relative error of at most 0.001.
Values are sent between devices in bfloat16 or wider.
A program may use at most 1.5 GiB of HBM per device.

v0:
```python
import functools

import jax
import jax.numpy as jnp
from jax import lax
from jax.experimental import pallas as pl
from jax.experimental.pallas import tpu as pltpu
from jax.sharding import PartitionSpec as P

MESH = pl.DeviceIdType.MESH
TILE = 16
NB = 256
HB = NB // 2
KC = 3072
XC = 1536
BUCKETS = (352, 416, 448) + tuple(range(480, 673, 16)) + (704, 736, 784)
PER = 4
LAST = 5
OFFS, LONE_TILE, LONE_ROW, LONE_SLOT, LONE_SOURCE, MERGE = 50, 54, 55, 56, 57, 64


def fused_kernel(rows, table_ref, x_ref, w_ref, out, *scratch):
    (xp, lone, wbuf, part, ra, sb, so, rb, xsem, wsem, send_a, recv_a, send_b, recv_b, send_c, recv_c, send_e, recv_e,
     send_d, recv_d, *stages) = scratch
    depth, cols = w_ref.shape
    blocks = cols // NB
    half = rows // 2
    ns = len(stages)
    me = lax.axis_index("tp")
    core = lax.rem(me, 2)
    chip = me // 2
    sibling = {"tp": me + 1 - 2 * core}
    peer = {"tp": lax.rem(me + 2, 4)}
    nk = depth // KC
    nx = depth // XC
    per = nx // nk

    def x_copy(n):
        return pltpu.make_async_copy(x_ref.at[:, :, pl.ds(n * XC, XC)], stages[n % ns], xsem.at[n % ns])

    def w_copy(b, k):
        s = lax.rem(b, 2)
        deep = pl.ds(pl.multiple_of(k * KC, KC), KC)
        return pltpu.make_async_copy(w_ref.at[deep, pl.ds(pl.multiple_of(b * NB, NB), NB)], wbuf.at[s, deep], wsem.at[s, k])

    def remote(src, dst, ssem, rsem, to):
        return pltpu.make_async_remote_copy(src_ref=src, dst_ref=dst, send_sem=ssem, recv_sem=rsem, device_id=to, device_id_type=MESH)

    def copy_a(b):
        s = lax.rem(b, 2)
        return remote(part.at[s, 1 - core], ra.at[s], send_a.at[s], recv_a.at[s], sibling)

    def copy_b(b):
        s, r = lax.rem(b, 4), lax.rem(b, 8)
        return remote(sb.at[s], rb.at[r], send_b.at[s], recv_b.at[r], peer)

    def copy_c(b):
        r = lax.rem(b, 8)
        return remote(out.at[b, core, chip], out.at[b, core, chip], send_c.at[r], recv_c.at[r], peer)

    def copy_e(b):
        r = lax.rem(b, 8)
        return remote(out.at[b, core, chip], out.at[b, core, chip], send_e.at[r], recv_e.at[r], sibling)

    def copy_d(b):
        r = lax.rem(b, 8)
        return remote(out.at[b, core, 1 - chip], out.at[b, core, 1 - chip], send_d.at[r], recv_d.at[r], sibling)

    for n in range(ns):
        x_copy(n).start()
        if n % per == per - 1:
            w_copy(0, n // per).start()

    barrier = pltpu.get_barrier_semaphore()
    for other in (sibling, peer):
        pl.semaphore_signal(barrier, inc=1, device_id=other, device_id_type=MESH)
    pl.semaphore_wait(barrier, 2)

    row = lax.broadcasted_iota(jnp.int32, (TILE, XC), 0)

    def pack(n):
        stage = stages[n % ns]
        x_copy(n).wait()
        if n == nx - 1:
            for k in range(nk):
                w_copy(1, k).start()
        first = stage[table_ref[LONE_SOURCE]][0:1, :].astype(jnp.float32)
        lone[...] = jnp.broadcast_to(first, (TILE, XC)).astype(lone.dtype)

        def tile(t, carry):
            at = pl.ds(pl.multiple_of(t * TILE, TILE), TILE)
            xp[at, n * XC:(n + 1) * XC] = jnp.where(row + 1 == table_ref[MERGE + t], lone[...], stage[table_ref[t]])
            return carry

        lax.fori_loop(0, rows // TILE, tile, 0)
        if n + ns < nx:
            x_copy(n + ns).start()
            if (n + ns) % per == per - 1:
                w_copy(0, (n + ns) // per).start()

    def pack_for(k):
        for n in range(k * per, (k + 1) * per):
            pack(n)

    def reduce_on(i):
        @pl.when(jnp.logical_and(i >= 1, i - 1 < blocks))
        def _():
            b = i - 1
            s, q = lax.rem(b, 2), lax.rem(b, 4)
            copy_a(b).wait()
            there = pl.ds(pl.multiple_of((1 - chip) * half, 8), half)
            here = pl.ds(pl.multiple_of(chip * half, 8), half)
            sb[q] = part[s, core, there, :] + ra[s, there, :]
            so[q] = part[s, core, here, :] + ra[s, here, :]
            copy_b(b).start()

    def finish(i):
        @pl.when(jnp.logical_and(i >= 2, i - 2 < blocks))
        def _():
            b = i - 2
            copy_b(b).wait()
            out[b, core, chip] = (so[lax.rem(b, 4)] + rb[lax.rem(b, 8)]).astype(out.dtype)
            copy_c(b).start()
            copy_e(b).start()

        @pl.when(jnp.logical_and(i >= 4, i - 4 < blocks))
        def _():
            copy_c(i - 4).wait()
            copy_d(i - 4).start()

        @pl.when(jnp.logical_and(i >= 5, i - 5 < blocks))
        def _():
            copy_e(i - 5).wait()
            copy_d(i - 5).wait()

    def step(j, carry):
        i, k = j // nk, lax.rem(j, nk)
        for early in range(nk):
            pl.when(j == early)(functools.partial(pack_for, early))

        @pl.when(k == jnp.where(i <= 3, 1, 2))
        def _():
            reduce_on(i)

        @pl.when(k == nk - 1)
        def _():
            finish(i)

        @pl.when(i < blocks)
        def _():
            @pl.when(jnp.logical_and(i >= 1, i + 1 < blocks))
            def _():
                w_copy(i + 1, k).start()

            w_copy(i, k).wait()
            s = lax.rem(i, 2)
            deep = pl.ds(pl.multiple_of(k * KC, KC), KC)
            split = rows // (2 * TILE) * TILE
            for part_rows in (slice(0, split), slice(split, rows)):
                prod = jnp.dot(xp[part_rows, deep], wbuf[s, deep, :], preferred_element_type=jnp.float32)
                for h in range(2):
                    part[s, h, part_rows] = jnp.where(k == 0, 0.0, part[s, h, part_rows]) + prod[:, h * HB:(h + 1) * HB]

            @pl.when(k == nk - 1)
            def _():
                copy_a(i).start()

        return carry

    lax.fori_loop(0, nk * (blocks + LAST), step, 0)


def unpack_kernel(lens_ref, table_ref, packed, y_ref, spread, osem):
    slots = lens_ref.shape[0]
    chunks, tokens, width = spread.shape
    slot_tiles = tokens // slots // TILE
    row = lax.broadcasted_iota(jnp.int32, (TILE, HB), 0)

    def store(c):
        return pltpu.make_async_copy(spread.at[c], y_ref.at[:, pl.ds(pl.multiple_of(c * width, width), width)], osem.at[c])

    def chunk(c, carry):
        def move(source, target, count, length=None):
            source = pl.multiple_of(source * TILE, TILE)
            target = pl.multiple_of(target * TILE, TILE)
            for j in range(width // HB):
                piece = packed[c * PER + j // 2, j % 2, pl.ds(source, count * TILE), :]
                if length is not None:
                    piece = jnp.where(row < length, piece, jnp.zeros_like(piece))
                spread[c, pl.ds(target, count * TILE), j * HB:(j + 1) * HB] = piece

        def clear(target, count):
            at = pl.ds(pl.multiple_of(target * TILE, TILE), count * TILE)
            spread[c, at, :] = jnp.zeros((count * TILE, width), spread.dtype)

        @pl.loop(0, slots)
        def _(s):
            merged = jnp.logical_and(table_ref[LONE_TILE] > 0, table_ref[LONE_SLOT] == s)
            length = jnp.where(merged, 0, lens_ref[s])
            full = lax.div(length, TILE)
            used = lax.div(length + TILE - 1, TILE)
            source, target = table_ref[OFFS + s], s * slot_tiles
            quads = lax.div(full, 4)
            empty = lax.div(used + 3, 4)

            @pl.loop(0, quads)
            def _(t):
                move(source + 4 * t, target + 4 * t, 4)

            @pl.loop(quads * 4, full)
            def _(t):
                move(source + t, target + t, 1)

            @pl.when(full < used)
            def _():
                move(source + full, target + full, 1, length - full * TILE)

            @pl.loop(used, empty * 4)
            def _(t):
                clear(target + t, 1)

            @pl.loop(empty, slot_tiles // 4)
            def _(t):
                clear(target + 4 * t, 4)

        @pl.when(table_ref[LONE_TILE] > 0)
        def _():
            source = pl.multiple_of((table_ref[LONE_TILE] - 1) * TILE, TILE)
            target = pl.multiple_of(table_ref[LONE_SLOT] * (slot_tiles * TILE), TILE)
            for j in range(width // HB):
                piece = packed[c * PER + j // 2, j % 2, pl.ds(source, TILE), :].astype(jnp.float32)
                line = jnp.sum(jnp.where(row == table_ref[LONE_ROW], piece, 0.0), axis=0, keepdims=True)
                spread[c, pl.ds(target, TILE), j * HB:(j + 1) * HB] = jnp.where(row == 0, line, 0.0).astype(spread.dtype)

        store(c).start()
        return carry

    lax.fori_loop(0, chunks, chunk, 0)
    for c in range(chunks):
        store(c).wait()


def branch(index, rows, x_loc, w_loc, lengths, table):
    tokens, depth = x_loc.shape
    cols = w_loc.shape[1]
    blocks = cols // NB
    half = rows // 2
    f32, bf16 = jnp.float32, x_loc.dtype
    dma = pltpu.SemaphoreType.DMA
    buffers = 4 if rows <= 704 else 3 if rows <= 736 else 2
    grant = 2 * (rows * depth + buffers * tokens * XC + TILE * XC + 2 * depth * NB) + 4 * 14 * rows * HB + 500_000
    packed = pl.pallas_call(
        functools.partial(fused_kernel, rows),
        out_shape=pltpu.VMEM((blocks, 2, 2, half, HB), bf16),
        in_specs=[pl.BlockSpec(memory_space=pltpu.SMEM), pl.BlockSpec(memory_space=pl.ANY), pl.BlockSpec(memory_space=pl.ANY)],
        out_specs=pl.BlockSpec(memory_space=pltpu.VMEM),
        scratch_shapes=[
            pltpu.VMEM((rows, depth), bf16),
            pltpu.VMEM((TILE, XC), bf16),
            pltpu.VMEM((2, depth, NB), bf16),
            pltpu.VMEM((2, 2, rows, HB), f32),
            pltpu.VMEM((2, rows, HB), f32),
            pltpu.VMEM((4, half, HB), f32),
            pltpu.VMEM((4, half, HB), f32),
            pltpu.VMEM((8, half, HB), f32),
            dma((buffers,)), dma((2, depth // KC)), dma((2,)), dma((2,)), dma((4,)), dma((8,)),
            dma((8,)), dma((8,)), dma((8,)), dma((8,)), dma((8,)), dma((8,)),
            *[pltpu.VMEM((tokens // TILE, TILE, XC), bf16)] * buffers,
        ],
        compiler_params=pltpu.CompilerParams(collective_id=index, has_side_effects=True, vmem_limit_bytes=grant),
        cost_estimate=pl.CostEstimate(flops=2 * rows * depth * cols, bytes_accessed=2 * depth * cols, transcendentals=0),
        name=f"fused_{rows}",
    )(table, x_loc.reshape(tokens // TILE, TILE, depth), w_loc)
    packed = packed.reshape(blocks, 2, rows, HB)
    chunks = blocks // PER
    return pl.pallas_call(
        unpack_kernel,
        out_shape=jax.ShapeDtypeStruct((tokens, cols), bf16),
        in_specs=[pl.BlockSpec(memory_space=pltpu.SMEM), pl.BlockSpec(memory_space=pltpu.SMEM), pl.BlockSpec(memory_space=pltpu.VMEM)],
        out_specs=pl.BlockSpec(memory_space=pl.ANY),
        scratch_shapes=[
            pltpu.VMEM((chunks, tokens, PER * NB), bf16),
            dma((chunks,)),
        ],
        compiler_params=pltpu.CompilerParams(vmem_limit_bytes=27_000_000),
        cost_estimate=pl.CostEstimate(flops=0, bytes_accessed=2 * (rows + tokens) * cols, transcendentals=0),
        name=f"unpack_{rows}",
    )(lengths, table, packed)


def table_kernel(tokens, lens_ref, table_ref, index_ref):
    slots = lens_ref.shape[0]
    slot_tiles = tokens // slots // TILE
    lens = [lens_ref[s] for s in range(slots)]
    lone = jnp.int32(slots - 1)
    for s in reversed(range(slots - 1)):
        lone = jnp.where(lens[s] == 1, s, lone)
    rest = [lax.rem(lens[s], TILE) for s in range(slots)]
    host = jnp.int32(-1)
    for s in reversed(range(slots)):
        host = jnp.where(jnp.logical_and(lone != s, rest[s] != 0), s, host)
    offs, total = [], jnp.int32(0)
    lone_tile, lone_row = jnp.int32(0), jnp.int32(0)
    for s in range(slots):
        offs.append(total)
        tiles = jnp.where(jnp.logical_and(host >= 0, lone == s), 0, lax.div(lens[s] + (TILE - 1), TILE))
        total = total + tiles
        lone_tile = jnp.where(host == s, total, lone_tile)
        lone_row = jnp.where(host == s, rest[s], lone_row)

    def tile(t, carry):
        source = t
        for s in range(1, slots):
            source = jnp.where(t >= offs[s], s * slot_tiles + t - offs[s], source)
        table_ref[t] = jnp.where(t < total, source, 0)
        table_ref[MERGE + t] = jnp.where(t + 1 == lone_tile, lone_row + 1, 0)
        return carry

    lax.fori_loop(0, OFFS, tile, 0)
    for s in range(slots):
        table_ref[OFFS + s] = offs[s]
    table_ref[LONE_TILE] = lone_tile
    table_ref[LONE_ROW] = lone_row
    table_ref[LONE_SLOT] = lone
    table_ref[LONE_SOURCE] = lone * slot_tiles
    index = jnp.int32(0)
    for size in BUCKETS[:-1]:
        index = index + (total * TILE > size).astype(jnp.int32)
    index_ref[0] = index


def make_table(lengths, tokens):
    smem = pl.BlockSpec(memory_space=pltpu.SMEM)
    return pl.pallas_call(
        functools.partial(table_kernel, tokens),
        out_shape=(jax.ShapeDtypeStruct((128,), jnp.int32), jax.ShapeDtypeStruct((1,), jnp.int32)),
        in_specs=[smem],
        out_specs=(smem, smem),
        name="table",
    )(lengths)


def solution(mesh):
    def local_part(x_loc, w_loc, lengths):
        table, index = make_table(lengths, x_loc.shape[0])
        return lax.switch(index[0], [functools.partial(branch, j, rows) for j, rows in enumerate(BUCKETS)], x_loc, w_loc, lengths, table)

    return jax.shard_map(local_part, mesh=mesh, in_specs=(P("data", "tp"), P("tp", None), P("data")), out_specs=P("data", None), check_vma=False)
```

profile of v0, /device:TPU:0, one launch (start us, length us, event | category | flops | bytes accessed | tf_op | source)
XLA Modules:
  0.0 274.8 jit_solution(16272829066251426226)
XLA Ops:
  0.0 1.8 table.1
  2.4 272.1 %conditional.1 = (bf16[1024,12288]{1,0:T(8,128)(2,1)}) conditional(s32[]{:T(128)} %bitcast.38, (bf16[1024,12288]{1,0:T(8,128)(2,1)}, s32[128]{0:T(128)S(1)}, bf16[12288,12288]{1,0:T(8,128)(2,1)}, s32[4]{0:T(128)}) %tuple.62, (bf16[1024,12288]{1,0:T(8,128)(2,1)}, s32[128]{0:T(128)S(1)}, ...), branch_computations={%region_0.0_spmd, %region_1.0_spmd, %region_2.0_spmd, %region_3.0_... | conditional | flops 236760072192 | bytes 346423392 | solution.py:346
  2.7 0.0 copy-start.11
  2.7 262.0 %fused_608.1 = bf16[48,2,2,304,128]{4,3,2,1,0:T(8,128)(2,1)S(1)} custom-call(s32[128]{0:T(128)S(1)} %get-tuple-element.222.table_ref, bf16[64,16,12288]{2,1,0:T(8,128)(2,1)} %bitcast.69, bf16[12288,12288]{1,0:T(8,128)(2,1)} %get-tuple-element.326.w_ref), custom_call_target="tpu_custom_call" | custom-call | flops 183609851904 | bytes 301989888 | tf_op jit(solution)/shard_map/cond/branch_11_fun/fused_608/pallas_call | solution.py:252
  264.7 0.0 copy-done.11
  264.7 9.6 %unpack_608.1 = bf16[1024,12288]{1,0:T(8,128)(2,1)} custom-call(s32[4]{0:T(128)S(1)} %copy-done.11, s32[128]{0:T(128)S(1)} %get-tuple-element.222.table_ref, bf16[48,2,608,128]{3,2,1,0:T(8,128)(2,1)S(1)} %bitcast.46), custom_call_target="tpu_custom_call" | custom-call | bytes 40108032 | tf_op jit(solution)/shard_map/cond/branch_11_fun/unpack_608/pallas_call | solution.py:276
Async XLA Ops:
  2.7 262.0 %copy-start.11 = (s32[4]{0:T(128)S(1)}, s32[4]{0:T(128)}, u32[]{:S(2)}) copy-start(s32[4]{0:T(128)} %get-tuple-element.221.lens_ref) | copy-start | bytes 52 | tf_op jit(solution)/shard_map/cond
where the time goes:
time: 274 us; the launch traced here: 275 us
  Pallas kernels  273 us (100%)
    pallas_call x1, Pallas kernels, branch(): pl.pallas_call(functools.partial(fused_kernel, rows), out_shape=pltpu.VME...  262 us
    pallas_call x1, Pallas kernels, branch(): pl.pallas_call(unpack_kernel, out_shape=jax.ShapeDtypeStruct((tokens, col...  9.59 us

commit v1 on v0

--- a/solution.py
+++ b/solution.py
@@ -11,12 +11,15 @@
 TILE = 16
 NB = 256
 HB = NB // 2
-KC = 3072
 XC = 1536
-BUCKETS = (352, 416, 448) + tuple(range(480, 673, 16)) + (704, 736, 784)
+BUCKETS = (352, 416, 448) + tuple(range(480, 753, 16)) + (784,)
 PER = 4
 LAST = 5
 OFFS, LONE_TILE, LONE_ROW, LONE_SLOT, LONE_SOURCE, MERGE = 50, 54, 55, 56, 57, 64
+
+
+def chunk_depth(rows):
+    return 6144 if rows <= 480 else 3072
 
 
 def fused_kernel(rows, table_ref, x_ref, w_ref, out, *scratch):
@@ -31,7 +34,8 @@
     chip = me // 2
     sibling = {"tp": me + 1 - 2 * core}
     peer = {"tp": lax.rem(me + 2, 4)}
-    nk = depth // KC
+    kc = chunk_depth(rows)
+    nk = depth // kc
     nx = depth // XC
     per = nx // nk
 
@@ -40,7 +44,7 @@
 
     def w_copy(b, k):
         s = lax.rem(b, 2)
-        deep = pl.ds(pl.multiple_of(k * KC, KC), KC)
+        deep = pl.ds(pl.multiple_of(k * kc, kc), kc)
         return pltpu.make_async_copy(w_ref.at[deep, pl.ds(pl.multiple_of(b * NB, NB), NB)], wbuf.at[s, deep], wsem.at[s, k])
 
     def remote(src, dst, ssem, rsem, to):
@@ -138,7 +142,7 @@
         for early in range(nk):
             pl.when(j == early)(functools.partial(pack_for, early))
 
-        @pl.when(k == jnp.where(i <= 3, 1, 2))
+        @pl.when(k == jnp.where(i <= 3, 1, min(2, nk - 1)))
         def _():
             reduce_on(i)
 
@@ -154,7 +158,7 @@
 
             w_copy(i, k).wait()
             s = lax.rem(i, 2)
-            deep = pl.ds(pl.multiple_of(k * KC, KC), KC)
+            deep = pl.ds(pl.multiple_of(k * kc, kc), kc)
             split = rows // (2 * TILE) * TILE
             for part_rows in (slice(0, split), slice(split, rows)):
                 prod = jnp.dot(xp[part_rows, deep], wbuf[s, deep, :], preferred_element_type=jnp.float32)
@@ -263,7 +267,7 @@
             pltpu.VMEM((4, half, HB), f32),
             pltpu.VMEM((4, half, HB), f32),
             pltpu.VMEM((8, half, HB), f32),
-            dma((buffers,)), dma((2, depth // KC)), dma((2,)), dma((2,)), dma((4,)), dma((8,)),
+            dma((buffers,)), dma((2, depth // chunk_depth(rows))), dma((2,)), dma((2,)), dma((4,)), dma((8,)),
             dma((8,)), dma((8,)), dma((8,)), dma((8,)), dma((8,)), dma((8,)),
             *[pltpu.VMEM((tokens // TILE, TILE, XC), bf16)] * buffers,
         ],

time: 274 us -> 262 us (0.956)
  the two profiles are of different devices: /device:TPU:0 before, /device:TPU:5 now
where the time goes in v1:
time: 262 us; the launch traced here: 261 us
  Pallas kernels  260 us (99%)
    pallas_call x1, Pallas kernels, branch(): pl.pallas_call(functools.partial(fused_kernel, rows), out_shape=pltpu.VME...  248 us
    pallas_call x1, Pallas kernels, branch(): pl.pallas_call(unpack_kernel, out_shape=jax.ShapeDtypeStruct((tokens, col...  9.58 us

profile of v1, /device:TPU:5, one launch (start us, length us, event | category | flops | bytes accessed | tf_op | source)
XLA Modules:
  0.0 261.2 jit_solution(15249454757389338277)
XLA Ops:
  0.0 1.8 table.1
  2.4 258.6 %conditional.1 = (bf16[1024,12288]{1,0:T(8,128)(2,1)}) conditional(s32[]{:T(128)} %bitcast.44, (bf16[1024,12288]{1,0:T(8,128)(2,1)}, s32[128]{0:T(128)S(1)}, bf16[12288,12288]{1,0:T(8,128)(2,1)}, s32[4]{0:T(128)}) %tuple.71, (bf16[1024,12288]{1,0:T(8,128)(2,1)}, s32[128]{0:T(128)S(1)}, ...), branch_computations={%region_0.0_spmd, %region_1.0_spmd, %region_2.0_spmd, %region_3.0_... | conditional | flops 236760072192 | bytes 346423392 | solution.py:350
  2.7 0.0 copy-start.9
  2.7 248.2 %fused_576.1 = bf16[48,2,2,288,128]{4,3,2,1,0:T(8,128)(2,1)S(1)} custom-call(s32[128]{0:T(128)S(1)} %get-tuple-element.241.table_ref, bf16[64,16,12288]{2,1,0:T(8,128)(2,1)} %bitcast.76, bf16[12288,12288]{1,0:T(8,128)(2,1)} %get-tuple-element.372.w_ref), custom_call_target="tpu_custom_call" | custom-call | flops 173946175488 | bytes 301989888 | tf_op jit(solution)/shard_map/cond/branch_9_fun/fused_576/pallas_call | solution.py:256
  250.9 0.0 copy-done.9
  250.9 9.6 %unpack_576.1 = bf16[1024,12288]{1,0:T(8,128)(2,1)} custom-call(s32[4]{0:T(128)S(1)} %copy-done.9, s32[128]{0:T(128)S(1)} %get-tuple-element.241.table_ref, bf16[48,2,576,128]{3,2,1,0:T(8,128)(2,1)S(1)} %bitcast.57), custom_call_target="tpu_custom_call" | custom-call | bytes 39321600 | tf_op jit(solution)/shard_map/cond/branch_9_fun/unpack_576/pallas_call | solution.py:280
Async XLA Ops:
  2.7 248.2 %copy-start.9 = (s32[4]{0:T(128)S(1)}, s32[4]{0:T(128)}, u32[]{:S(2)}) copy-start(s32[4]{0:T(128)} %get-tuple-element.240.lens_ref) | copy-start | bytes 52 | tf_op jit(solution)/shard_map/cond
